TPU v7x, 32 devices: a whole 2x2x4 slice. The times are simulated.
32 devices in a mesh: space: 8 (over z, y), level: 4 (over x, core).
Axes of the slice: x: 2, y: 2, z: 4, core: 2. Of those that a mesh axis runs over, the one named last changes fastest.
Arguments:
- grid_latent: bfloat16 [4096, 512], P('space'), may hold values from -6 to 6
- mesh_latent: bfloat16 [4, 64, 512], P('level', 'space'), may hold values from -6 to 6
- grid_output_cotangent: bfloat16 [4096, 512], P('space'), may hold values from -6 to 6
- w_send: bfloat16 [512, 512], replicated, may hold values from -0.25 to 0.25
- w_recv: bfloat16 [512, 512], replicated, may hold values from -0.25 to 0.25
- output_weight: bfloat16 [512, 512], replicated, may hold values from -0.25 to 0.25
- hidden_layer_bias: float32 [512], replicated, may hold values from -4 to 4
- output_norm_gain: float32 [512], replicated, may hold values from 0.1 to 1.9
- edge_sender: int32 [4, 16384], P('level', 'space'), may hold values from 0 to 23
- edge_receiver: int32 [4, 16384], P('level', 'space'), may hold values from 0 to 511
- edge_live: int32 [4, 16384], P('level', 'space'), may hold values 0 or 1
Outputs:
- d_grid: float32 [4096, 512], P(('space', 'level'))
- d_mesh: float32 [4, 64, 512], P('level', 'space')
- d_w_send: bfloat16 [512, 512], replicated
- d_w_recv: bfloat16 [512, 512], replicated
- d_w_out: bfloat16 [512, 512], replicated
- d_bias: float32 [512], replicated
- d_gain: float32 [512], replicated
All inputs are finite; a program needn't handle non-finite values. No bound on the sum of `edge_live` on one device may be relied on, other than what follows from the above.
Results may differ from a plain program's by a relative error of at most 0.012.
Values may be sent and summed in bfloat16 or wider, within the bound.
No kernel may reach another device: no remote copies, remote signals or barrier semaphores. Data moves between devices by JAX's collectives and lax.ppermute only.
A program may use at most 64 MiB of HBM per device.

v0:
```python
import jax
import jax.numpy as jnp
from jax import lax
from jax.sharding import PartitionSpec as P


def with_halo(cells, sides, width):
    for axis, dim in sides:
        count = lax.axis_size(axis)
        ends = count - 1
        head = lax.slice_in_dim(cells, 0, width, axis=dim)
        tail = lax.slice_in_dim(cells, cells.shape[dim] - width, cells.shape[dim], axis=dim)
        cells = jnp.concatenate(
            [
                lax.ppermute(tail, axis, [(i, (i + 1) % count) for i in range(ends)]),
                cells,
                lax.ppermute(head, axis, [((i + 1) % count, i) for i in range(ends)]),
            ],
            axis=dim,
        )
    return cells


def from_behind(block, axis, distance):
    devices = range(lax.axis_size(axis))
    route = [(i - distance, i) for i in devices if i - distance in devices]
    return lax.ppermute(block, axis, route)


def edge_reverse_step(
    sending_rows,
    receiver_rows,
    cotangent_lines,
    slot_active_flags,
    output_weight,
    hidden_layer_bias,
    output_norm_gain,
):
    preact = sending_rows + receiver_rows + hidden_layer_bias
    hidden = jax.nn.silu(preact).astype(jnp.bfloat16)
    outer = jnp.dot(hidden, output_weight, preferred_element_type=jnp.float32)
    center = outer - jnp.mean(outer, axis=-1, keepdims=True)
    inv_scale = lax.rsqrt(jnp.mean(center * center, axis=-1, keepdims=True) + 1e-05)
    normed = center * inv_scale
    incoming_gradient = cotangent_lines.astype(jnp.float32) * slot_active_flags[:, None].astype(
        jnp.float32
    )
    scaled = incoming_gradient * output_norm_gain
    d_outer = inv_scale * (
        scaled
        - jnp.mean(scaled, axis=-1, keepdims=True)
        - normed * jnp.mean(scaled * normed, axis=-1, keepdims=True)
    )
    d_outer_b = d_outer.astype(jnp.bfloat16)
    w_out_grad = jnp.dot(hidden.T, d_outer_b, preferred_element_type=jnp.float32)
    d_hidden = jnp.dot(d_outer_b, output_weight.T, preferred_element_type=jnp.float32)
    sigmoid = jax.nn.sigmoid(preact)
    preactivation_gradient = d_hidden * sigmoid * (1.0 + preact * (1.0 - sigmoid))
    return (
        preactivation_gradient,
        w_out_grad,
        jnp.sum(preactivation_gradient, axis=0),
        jnp.sum(incoming_gradient * normed, axis=0),
    )


def body(
    grid_latent,
    mesh_latent,
    grid_output_cotangent,
    w_send,
    w_recv,
    output_weight,
    hidden_layer_bias,
    output_norm_gain,
    edge_sender,
    edge_receiver,
    edge_live,
):
    shards = lax.axis_size("space")
    width = grid_latent.shape[1]
    grid_rows = grid_latent.shape[0]
    mesh_rows = mesh_latent.shape[1]
    slots = edge_sender.shape[1]
    sender_local = edge_sender[0]
    receiver_index = edge_receiver[0]
    band = lax.axis_index("space")
    window = sender_local // mesh_rows
    target = band + window - 1
    inside = (target >= 0) & (target < shards)
    window = jnp.where(inside, window, 1)
    table_row = window * mesh_rows + sender_local % mesh_rows
    proj_send = jnp.dot(mesh_latent[0], w_send, preferred_element_type=jnp.float32).astype(
        jnp.bfloat16
    )
    projected_receiver = jnp.dot(grid_latent, w_recv, preferred_element_type=jnp.float32)
    table = with_halo(proj_send, (("space", 0),), mesh_rows)
    sending_rows = table[table_row]
    block = 512
    blocks = slots // block

    def run_block(operands):
        rows_send, rows_recv, rows_cot, rows_live = operands
        return edge_reverse_step(
            rows_send.astype(jnp.float32),
            rows_recv,
            rows_cot,
            rows_live,
            output_weight,
            hidden_layer_bias,
            output_norm_gain,
        )

    operands = (
        sending_rows.reshape(blocks, block, width),
        projected_receiver[receiver_index].reshape(blocks, block, width),
        grid_output_cotangent[receiver_index].reshape(blocks, block, width),
        edge_live[0].reshape(blocks, block),
    )
    d_pre_blocks, wout_blocks, bias_blocks, gain_blocks = lax.map(run_block, operands)
    preactivation_gradient = d_pre_blocks.reshape(slots, width)
    output_weight_piece = jnp.sum(wout_blocks, axis=0)
    bias_piece = jnp.sum(bias_blocks, axis=0)
    gain_piece = jnp.sum(gain_blocks, axis=0)
    table_grads = jax.ops.segment_sum(preactivation_gradient, table_row, num_segments=3 * mesh_rows)
    below = table_grads[:mesh_rows]
    above = table_grads[2 * mesh_rows :]
    from_below = from_behind(above, "space", 1)
    from_above = from_behind(below, "space", -1)
    mesh_acc = table_grads[mesh_rows : 2 * mesh_rows] + from_below + from_above
    grid_local = jax.ops.segment_sum(preactivation_gradient, receiver_index, num_segments=grid_rows)
    share = grid_rows // lax.axis_size("level")
    offset = lax.axis_index("level") * share
    grid_acc = lax.psum_scatter(
        grid_local.astype(jnp.bfloat16), "level", scatter_dimension=0, tiled=True
    )
    grid_part = lax.dynamic_slice_in_dim(grid_latent, offset, share, 0)
    mesh_sum = mesh_acc.astype(jnp.bfloat16)
    d_mesh = jnp.dot(mesh_sum, w_send.T, preferred_element_type=jnp.float32)[None]
    d_grid = jnp.dot(grid_acc, w_recv.T, preferred_element_type=jnp.float32)
    wsend_part = jnp.dot(mesh_latent[0].T, mesh_sum, preferred_element_type=jnp.float32)
    wrecv_part = jnp.dot(grid_part.T, grid_acc, preferred_element_type=jnp.float32)
    totals = lax.psum(
        (wsend_part, wrecv_part, output_weight_piece, bias_piece, gain_piece), ("space", "level")
    )
    d_w_send = totals[0].astype(jnp.bfloat16)
    d_w_recv = totals[1].astype(jnp.bfloat16)
    d_w_out = totals[2].astype(jnp.bfloat16)
    d_bias = totals[3]
    d_gain = totals[4]
    return (d_grid, d_mesh, d_w_send, d_w_recv, d_w_out, d_bias, d_gain)


def solution(mesh):
    return jax.shard_map(
        body,
        mesh=mesh,
        in_specs=(
            P("space", None),
            P("level", "space", None),
            P("space", None),
            P(),
            P(),
            P(),
            P(),
            P(),
            P("level", "space"),
            P("level", "space"),
            P("level", "space"),
        ),
        out_specs=(P(("space", "level"), None), P("level", "space", None), P(), P(), P(), P(), P()),
        check_vma=False,
    )
```

profile of v0, /device:TPU:0, one launch (start us, length us, event | category | flops | bytes accessed | tf_op | source)
XLA Modules:
  0.0 218.6 jit_solution(9644242598406611209)
XLA Ops:
  7.2 1.3 convolution_convert_fusion
  8.5 1.3 collective-permute-start.1
  9.8 5.5 %collective-permute-start = (bf16[8,512]{1,0:T(8,128)(2,1)S(1)}, bf16[8,512]{1,0:T(8,128)(2,1)S(1)}, u32[]{:S(2)}, u32[]{:S(2)}) collective-permute-start(bf16[8,512]{1,0:T(8,128)(2,1)S(1)} %convolution_convert_fusion), channel_id=1, source_target_pairs={{0,4},{4,8},{8,12},{12,16},{16,20},{20,24},{24,28},{1,5},{5,9},{9,... | collective-permute-start | bytes 24584 | tf_op jit(solution)/shard_map/ppermute | solution.py:15
  15.3 0.7 compare_select_fusion
  16.1 0.8 compare_select_fusion.1
  16.9 1.6 fusion.27
  18.5 0.5 broadcast.290
  19.1 1.4 reduce.3
  20.5 9.2 %gather_fusion.2 = bf16[2048,512]{1,0:T(8,128)(2,1)} fusion(bf16[512,512]{1,0:T(8,128)(2,1)S(1)} %copy-done, s32[2048]{0:T(1024)S(1)} %broadcast_clamp_fusion), kind=kCustom, calls=%fused_computation.2 | custom fusion | bytes 4202496 | tf_op jit(solution)/shard_map/gather | solution.py:117
  29.6 8.9 %gather_fusion.1 = f32[2048,512]{1,0:T(8,128)} fusion(f32[512,512]{1,0:T(8,128)S(1)} %fusion.27, s32[2048]{0:T(1024)S(1)} %broadcast_clamp_fusion), kind=kCustom, calls=%fused_computation.1 | custom fusion | bytes 8396800 | tf_op jit(solution)/shard_map/gather | solution.py:116
  38.6 9.2 %gather_fusion = bf16[2048,512]{1,0:T(8,128)(2,1)} fusion(bf16[24,512]{1,0:T(8,128)(2,1)S(1)} %pad_maximum_fusion, s32[2048]{0:T(1024)S(1)} %broadcast_clamp_fusion.1), kind=kCustom, calls=%fused_computation | custom fusion | bytes 4202496 | tf_op jit(solution)/shard_map/gather | solution.py:98
  47.8 37.2 %while.16 = (s32[]{:T(128)}, f32[4,512,512]{2,1,0:T(8,128)}, f32[4,512,512]{2,1,0:T(8,128)}, f32[4,512]{1,0:T(4,128)S(1)}, f32[4,512]{1,0:T(4,128)S(1)}, /*index...) while((s32[]{:T(128)}, f32[4,512,512]{2,1,0:T(8,128)}, ...), condition=%wide.region_7.8_spmd, body=%wide.region_0.7_spmd.sunk | while | flops 816840704 | bytes 18942132 | solution.py:120
  47.8 1.7 multiply_convert_fusion.2
  49.5 1.1 constant_dynamic-slice_fusion.2
  50.8 0.5 fusion.60
  51.5 0.5 fusion.61
  51.9 0.3 fusion.62
  52.3 1.6 fusion.63
  53.9 3.0 %bitcast_dynamic-update-slice_fusion.2 = (f32[4,512,512]{2,1,0:T(8,128)}, f32[512,512]{1,0:T(8,128)S(1)}) fusion(f32[4,512,512]{2,1,0:T(8,128)} %get-tuple-element.263, s32[]{:T(128)S(6)} %copy.34, f32[512]{0:T(512)S(1)} %get-tuple-element.284, f32[4,512,512]{2,1,0:T(8,128)} %get-tuple-element.283, bf16[4,512,512]{2,1,0:T(8,128)(2,1)} %get-tuple-element.282, ...), kind=kOutput, calls=%fused_computation.20.clone.1 | convolution fusion | flops 271319040 | bytes 4720644 | tf_op jit(solution)/shard_map/while/body/eval_jaxpr/dot_general | solution.py:56
  57.1 1.7 multiply_convert_fusion.2
  58.8 1.1 constant_dynamic-slice_fusion.2
  60.1 0.5 fusion.60
  60.8 0.5 fusion.61
  61.7 1.5 fusion.63
  63.2 3.1 %bitcast_dynamic-update-slice_fusion.2 = (f32[4,512,512]{2,1,0:T(8,128)}, f32[512,512]{1,0:T(8,128)S(1)}) fusion(f32[4,512,512]{2,1,0:T(8,128)} %get-tuple-element.263, s32[]{:T(128)S(6)} %copy.34, f32[512]{0:T(512)S(1)} %get-tuple-element.284, f32[4,512,512]{2,1,0:T(8,128)} %get-tuple-element.283, bf16[4,512,512]{2,1,0:T(8,128)(2,1)} %get-tuple-element.282, ...), kind=kOutput, calls=%fused_computation.20.clone.1 | convolution fusion | flops 271319040 | bytes 4720644 | tf_op jit(solution)/shard_map/while/body/eval_jaxpr/dot_general | solution.py:56
  66.4 1.7 multiply_convert_fusion.2
  68.1 1.1 constant_dynamic-slice_fusion.2
  69.4 0.5 fusion.60
  70.1 0.5 fusion.61
  71.0 1.5 fusion.63
  72.5 3.1 %bitcast_dynamic-update-slice_fusion.2 = (f32[4,512,512]{2,1,0:T(8,128)}, f32[512,512]{1,0:T(8,128)S(1)}) fusion(f32[4,512,512]{2,1,0:T(8,128)} %get-tuple-element.263, s32[]{:T(128)S(6)} %copy.34, f32[512]{0:T(512)S(1)} %get-tuple-element.284, f32[4,512,512]{2,1,0:T(8,128)} %get-tuple-element.283, bf16[4,512,512]{2,1,0:T(8,128)(2,1)} %get-tuple-element.282, ...), kind=kOutput, calls=%fused_computation.20.clone.1 | convolution fusion | flops 271319040 | bytes 4720644 | tf_op jit(solution)/shard_map/while/body/eval_jaxpr/dot_general | solution.py:56
  75.7 1.7 multiply_convert_fusion.2
  77.4 1.1 constant_dynamic-slice_fusion.2
  78.7 0.5 fusion.60
  79.4 0.5 fusion.61
  80.3 1.5 fusion.63
  81.7 3.0 %bitcast_dynamic-update-slice_fusion.2 = (f32[4,512,512]{2,1,0:T(8,128)}, f32[512,512]{1,0:T(8,128)S(1)}) fusion(f32[4,512,512]{2,1,0:T(8,128)} %get-tuple-element.263, s32[]{:T(128)S(6)} %copy.34, f32[512]{0:T(512)S(1)} %get-tuple-element.284, f32[4,512,512]{2,1,0:T(8,128)} %get-tuple-element.283, bf16[4,512,512]{2,1,0:T(8,128)(2,1)} %get-tuple-element.282, ...), kind=kOutput, calls=%fused_computation.20.clone.1 | convolution fusion | flops 271319040 | bytes 4720644 | tf_op jit(solution)/shard_map/while/body/eval_jaxpr/dot_general | solution.py:56
  84.9 13.5 %scatter_custom_fusion = f32[512,512]{1,0:T(8,128)S(1)} fusion(s32[2048]{0:T(1024)} %bitcast.107, f32[2048,512]{1,0:T(8,128)} %bitcast.108, f32[]{:T(128)} %constant.75.clone.1), kind=kCustom, calls=%fused_computation.35 | custom fusion | flops 1048576 | bytes 1049088 | tf_op jit(solution)/shard_map/scatter-add | solution.py:131
  98.4 0.9 convert_element_type.46
  99.3 13.2 %scatter_custom_fusion.1 = f32[24,512]{1,0:T(8,128)S(1)} fusion(s32[2048]{0:T(1024)S(1)} %bitcast.106, f32[2048,512]{1,0:T(8,128)} %bitcast.109, f32[]{:T(128)} %constant.75.clone.1), kind=kCustom, calls=%fused_computation.45 | custom fusion | flops 1048576 | bytes 49664 | tf_op jit(solution)/shard_map/scatter-add | solution.py:125
  112.6 4.8 %collective-permute-start.2 = (f32[8,512]{1,0:T(8,128)S(1)}, f32[8,512]{1,0:T(8,128)S(1)}, u32[]{:S(2)}, u32[]{:S(2)}) collective-permute-start(f32[8,512]{1,0:T(8,128)S(1)} %get-tuple-element.154), channel_id=1, source_target_pairs={{0,4},{4,8},{8,12},{12,16},{16,20},{20,24},{24,28},{1,5},{5,9},{9,... | collective-permute-start | bytes 49160 | tf_op jit(solution)/shard_map/ppermute | solution.py:27
  117.4 1.5 collective-permute-start.3
  118.9 3.8 %reduce_sum.81 = f32[512,512]{1,0:T(8,128)} reduce(f32[4,512,512]{2,1,0:T(8,128)} %get-tuple-element.73, f32[]{:T(128)} %constant.75.clone.1), dimensions={0}, to_apply=%region_13.14 | reduce | flops 786432 | bytes 5242884 | tf_op jit(solution)/shard_map/reduce_sum | solution.py:122
  123.4 0.9 convolution_bitcast_fusion.2
  124.3 1.3 fusion.14
  125.6 83.1 %all-reduce.2 = (bf16[512,512]{0,1:T(8,128)(2,1)}, bf16[512,512]{1,0:T(8,128)(2,1)}, bf16[512,512]{1,0:T(8,128)(2,1)}, f32[512]{0:T(512)}, f32[512]{0:T(512)}) all-reduce(f32[512,512]{0,1:T(8,128)S(1)} %convolution_bitcast_fusion.1, f32[512,512]{1,0:T(8,128)S(1)} %fusion.14, ...), channel_id=1, replica_groups=mesh['space'=8,'level'=4] {'space','level'}, use_global_device_ids=true, to_apply=%region_11.12 | all-reduce | flops 787456 | bytes 4726784 | tf_op jit(solution)/shard_map/psum | solution.py:143
  208.7 2.0 copy.21
  210.7 1.0 fusion.28
  (75 shorter events, 4.4 us)
Async XLA Ops:
  7.2 13.3 %copy-start = (bf16[512,512]{1,0:T(8,128)(2,1)S(1)}, bf16[512,512]{1,0:T(8,128)(2,1)}, u32[]{:S(2)}) copy-start(bf16[512,512]{1,0:T(8,128)(2,1)} %param.15) | copy-start | bytes 1572868
  7.2 117.1 %reduce-scatter.2.cloned.1.call-start = ((), (), s32[]{:S(2)}) async-start(), calls=%async_computation.1 | async-start | bytes 655360 | tf_op jit(solution)/shard_map/reduce_scatter | solution.py:134
  8.5 30.0 %collective-permute-start.1 = (bf16[8,512]{1,0:T(8,128)(2,1)S(1)}, bf16[8,512]{1,0:T(8,128)(2,1)S(1)}, u32[]{:S(2)}, u32[]{:S(2)}) collective-permute-start(bf16[8,512]{1,0:T(8,128)(2,1)S(1)} %convolution_convert_fusion), channel_id=1, source_target_pairs={{4,0},{8,4},{12,8},{16,12},{20,16},{24,20},{28,24},{5,1},{9,5},{13... | collective-permute-start | bytes 24584 | tf_op jit(solution)/shard_map/ppermute | solution.py:17
  9.8 28.7 %collective-permute-start = (bf16[8,512]{1,0:T(8,128)(2,1)S(1)}, bf16[8,512]{1,0:T(8,128)(2,1)S(1)}, u32[]{:S(2)}, u32[]{:S(2)}) collective-permute-start(bf16[8,512]{1,0:T(8,128)(2,1)S(1)} %convolution_convert_fusion), channel_id=1, source_target_pairs={{0,4},{4,8},{8,12},{12,16},{16,20},{20,24},{24,28},{1,5},{5,9},{9,... | collective-permute-start | bytes 24584 | tf_op jit(solution)/shard_map/ppermute | solution.py:15
  38.5 9.2 %copy-start.1 = (bf16[512,512]{1,0:T(8,128)(2,1)S(1)}, bf16[512,512]{1,0:T(8,128)(2,1)}, u32[]{:S(2)}) copy-start(bf16[512,512]{1,0:T(8,128)(2,1)} %param.18) | copy-start | bytes 1572868
  38.5 9.2 %copy-start.5 = (f32[512]{0:T(512)S(1)}, f32[512]{0:T(512)}, u32[]{:S(2)}) copy-start(f32[512]{0:T(512)} %param.20) | copy-start | bytes 6148
  38.5 9.2 %copy-start.6 = (f32[512]{0:T(512)S(1)}, f32[512]{0:T(512)}, u32[]{:S(2)}) copy-start(f32[512]{0:T(512)} %param.19) | copy-start | bytes 6148
  84.9 38.1 %copy-start.7 = (bf16[1,8,512]{2,1,0:T(8,128)(2,1)S(1)}, bf16[1,8,512]{2,1,0:T(8,128)(2,1)}, u32[]{:S(2)}) copy-start(bf16[1,8,512]{2,1,0:T(8,128)(2,1)} %param.14) | copy-start | bytes 24580
  98.4 25.0 %copy-start.2 = (bf16[512,512]{1,0:T(8,128)(2,1)S(1)}, bf16[512,512]{1,0:T(8,128)(2,1)}, u32[]{:S(2)}) copy-start(bf16[512,512]{1,0:T(8,128)(2,1)} %param.16) | copy-start | bytes 1572868
  112.6 10.1 %collective-permute-start.2 = (f32[8,512]{1,0:T(8,128)S(1)}, f32[8,512]{1,0:T(8,128)S(1)}, u32[]{:S(2)}, u32[]{:S(2)}) collective-permute-start(f32[8,512]{1,0:T(8,128)S(1)} %get-tuple-element.154), channel_id=1, source_target_pairs={{0,4},{4,8},{8,12},{12,16},{16,20},{20,24},{24,28},{1,5},{5,9},{9,... | collective-permute-start | bytes 49160 | tf_op jit(solution)/shard_map/ppermute | solution.py:27
  117.4 5.6 %collective-permute-start.3 = (f32[8,512]{1,0:T(8,128)S(1)}, f32[8,512]{1,0:T(8,128)S(1)}, u32[]{:S(2)}, u32[]{:S(2)}) collective-permute-start(f32[8,512]{1,0:T(8,128)S(1)} %get-tuple-element.155), channel_id=1, source_target_pairs={{4,0},{8,4},{12,8},{16,12},{20,16},{24,20},{28,24},{5,1},{9,5},{13... | collective-permute-start | bytes 49160 | tf_op jit(solution)/shard_map/ppermute | solution.py:27
  122.7 88.0 %copy-start.3 = (bf16[512,512]{1,0:T(8,128)(2,1)S(1)}, bf16[512,512]{1,0:T(8,128)(2,1)}, u32[]{:S(2)}) copy-start(bf16[512,512]{1,0:T(8,128)(2,1)} %param.17) | copy-start | bytes 1572868
  124.3 86.5 %copy-start.4 = (bf16[128,512]{1,0:T(8,128)(2,1)S(1)}, bf16[128,512]{1,0:T(8,128)(2,1)}, u32[]{:S(2)}) copy-start(bf16[128,512]{1,0:T(8,128)(2,1)} %reduce-scatter.2.cloned.1.call-done) | copy-start | bytes 393220
Sparse Core Ops, SparseCore 0:
  99.4 23.2 reduce-scatter.1
where the time goes:
time: 220 us; the launch traced here: 219 us
  blocking collectives  83.1 us (38%)
  other arithmetic  45.5 us (21%)
  local copies, waits for them, and re-layouts  35.4 us (16%)
  matrix products  26.6 us (12%)
  between operations  14.3 us (6%)
  starting transfers between devices  13.2 us (6%)
    psum x1, blocking collectives, body(): lax.psum((wsend_part, wrecv_part, output_weight_piece, bias_piece, gain_p...  83.1 us
    scatter-add x1, other arithmetic, body(): jax.ops.segment_sum(preactivation_gradient, receiver_index, num_segments=...  13.5 us
    scatter-add x1, other arithmetic, body(): jax.ops.segment_sum(preactivation_gradient, table_row, num_segments=3 * m...  13.2 us
    dot_general x4, matrix products, edge_reverse_step(): jnp.dot(d_outer_b, output_weight.T, preferred_element_type=jnp.float32)  12.2 us
    gather x1, local copies, waits for them, and re-layouts, body(): sending_rows = table[table_row]  9.18 us
    gather x1, local copies, waits for them, and re-layouts, body(): grid_output_cotangent[receiver_index].reshape(blocks, block, width)  9.15 us
    gather x1, local copies, waits for them, and re-layouts, body(): projected_receiver[receiver_index].reshape(blocks, block, width)  8.9 us
    convert_element_type x4, other arithmetic, edge_reverse_step(): hidden = jax.nn.silu(preact).astype(jnp.bfloat16)  6.68 us
  transfers between devices with their start and end apart: 5, of which 1 were waited for; matrix products, arithmetic and copies ran while one was open for 19% of the time, Pallas kernels for 0%

commit v1 on v0

--- a/solution.py
+++ b/solution.py
@@ -140,9 +140,8 @@
     d_grid = jnp.dot(grid_acc, w_recv.T, preferred_element_type=jnp.float32)
     wsend_part = jnp.dot(mesh_latent[0].T, mesh_sum, preferred_element_type=jnp.float32)
     wrecv_part = jnp.dot(grid_part.T, grid_acc, preferred_element_type=jnp.float32)
-    totals = lax.psum(
-        (wsend_part, wrecv_part, output_weight_piece, bias_piece, gain_piece), ("space", "level")
-    )
+    wrap_view_in = lambda frame: lax.psum(lax.psum(frame, "space"), "level")
+    totals = wrap_view_in((wsend_part, wrecv_part, output_weight_piece, bias_piece, gain_piece))
     d_w_send = totals[0].astype(jnp.bfloat16)
     d_w_recv = totals[1].astype(jnp.bfloat16)
     d_w_out = totals[2].astype(jnp.bfloat16)

time: 220 us -> 326 us (1.48)
  waiting for transfers between devices: 0.36 us -> 108 us
    psum x0 -> x1, waiting for transfers between devices: none -> 108 us  [body(): wrap_view_in = lambda frame: lax.psum(lax.psum(frame, 'space'), 'level')]
    psum x1 -> x2, blocking collectives: 83.1 us -> 80.7 us  [body(): wrap_view_in = lambda frame: lax.psum(lax.psum(frame, 'space'), 'level')]
  transfers between devices with their start and end apart: 5 -> 6, of which waited for: 1 -> 2; matrix products, arithmetic and copies ran while one was open for 19% -> 13% of each run, Pallas kernels for 0% -> 0%
where the time goes in v1:
time: 326 us; the launch traced here: 325 us
  waiting for transfers between devices  108 us (33%)
  blocking collectives  80.7 us (25%)
  other arithmetic  45.5 us (14%)
  local copies, waits for them, and re-layouts  34.4 us (11%)
  matrix products  28.6 us (9%)
  between operations  14.3 us (4%)
  starting transfers between devices  13.2 us (4%)
    psum x1, waiting for transfers between devices, body(): wrap_view_in = lambda frame: lax.psum(lax.psum(frame, 'space'), 'level')  108 us
    psum x2, blocking collectives, body(): wrap_view_in = lambda frame: lax.psum(lax.psum(frame, 'space'), 'level')  80.7 us
    scatter-add x1, other arithmetic, body(): jax.ops.segment_sum(preactivation_gradient, receiver_index, num_segments=...  13.5 us
    scatter-add x1, other arithmetic, body(): jax.ops.segment_sum(preactivation_gradient, table_row, num_segments=3 * m...  13.2 us
    dot_general x4, matrix products, edge_reverse_step(): jnp.dot(d_outer_b, output_weight.T, preferred_element_type=jnp.float32)  12.2 us
    gather x1, local copies, waits for them, and re-layouts, body(): sending_rows = table[table_row]  9.18 us
    gather x1, local copies, waits for them, and re-layouts, body(): grid_output_cotangent[receiver_index].reshape(blocks, block, width)  9.15 us
    gather x1, local copies, waits for them, and re-layouts, body(): projected_receiver[receiver_index].reshape(blocks, block, width)  8.9 us
  transfers between devices with their start and end apart: 6, of which 2 were waited for; matrix products, arithmetic and copies ran while one was open for 13% of the time, Pallas kernels for 0%

profile of v1, /device:TPU:0, one launch (start us, length us, event | category | flops | bytes accessed | tf_op | source)
XLA Modules:
  0.0 324.8 jit_solution(12237880396287006023)
XLA Ops:
  7.2 1.3 convolution_convert_fusion
  8.5 1.3 collective-permute-start.1
  9.8 5.5 %collective-permute-start = (bf16[8,512]{1,0:T(8,128)(2,1)S(1)}, bf16[8,512]{1,0:T(8,128)(2,1)S(1)}, u32[]{:S(2)}, u32[]{:S(2)}) collective-permute-start(bf16[8,512]{1,0:T(8,128)(2,1)S(1)} %convolution_convert_fusion), channel_id=1, source_target_pairs={{0,4},{4,8},{8,12},{12,16},{16,20},{20,24},{24,28},{1,5},{5,9},{9,... | collective-permute-start | bytes 24584 | tf_op jit(solution)/shard_map/ppermute | solution.py:15
  15.3 0.7 compare_select_fusion
  16.1 0.8 compare_select_fusion.1
  16.9 1.6 fusion.27
  18.5 0.5 broadcast.290
  19.1 1.4 reduce.3
  20.5 9.2 %gather_fusion.2 = bf16[2048,512]{1,0:T(8,128)(2,1)} fusion(bf16[512,512]{1,0:T(8,128)(2,1)S(1)} %copy-done, s32[2048]{0:T(1024)S(1)} %broadcast_clamp_fusion), kind=kCustom, calls=%fused_computation.2 | custom fusion | bytes 4202496 | tf_op jit(solution)/shard_map/gather | solution.py:117
  29.6 8.9 %gather_fusion.1 = f32[2048,512]{1,0:T(8,128)} fusion(f32[512,512]{1,0:T(8,128)S(1)} %fusion.27, s32[2048]{0:T(1024)S(1)} %broadcast_clamp_fusion), kind=kCustom, calls=%fused_computation.1 | custom fusion | bytes 8396800 | tf_op jit(solution)/shard_map/gather | solution.py:116
  38.6 9.2 %gather_fusion = bf16[2048,512]{1,0:T(8,128)(2,1)} fusion(bf16[24,512]{1,0:T(8,128)(2,1)S(1)} %pad_maximum_fusion, s32[2048]{0:T(1024)S(1)} %broadcast_clamp_fusion.1), kind=kCustom, calls=%fused_computation | custom fusion | bytes 4202496 | tf_op jit(solution)/shard_map/gather | solution.py:98
  47.8 37.2 %while.16 = (s32[]{:T(128)}, f32[4,512,512]{2,1,0:T(8,128)}, f32[4,512,512]{2,1,0:T(8,128)}, f32[4,512]{1,0:T(4,128)S(1)}, f32[4,512]{1,0:T(4,128)S(1)}, /*index...) while((s32[]{:T(128)}, f32[4,512,512]{2,1,0:T(8,128)}, ...), condition=%wide.region_7.8_spmd, body=%wide.region_0.7_spmd.sunk | while | flops 816840704 | bytes 18942132 | solution.py:120
  47.8 1.7 multiply_convert_fusion.2
  49.5 1.1 constant_dynamic-slice_fusion.2
  50.8 0.5 fusion.60
  51.5 0.5 fusion.61
  52.3 1.6 fusion.63
  53.9 3.0 bitcast_dynamic-update-slice_fusion.2
  57.1 1.7 multiply_convert_fusion.2
  58.8 1.1 constant_dynamic-slice_fusion.2
  60.1 0.5 fusion.60
  61.7 1.5 fusion.63
  63.2 3.1 bitcast_dynamic-update-slice_fusion.2
  66.4 1.7 multiply_convert_fusion.2
  68.1 1.1 constant_dynamic-slice_fusion.2
  69.4 0.5 fusion.60
  71.0 1.5 fusion.63
  72.5 3.1 bitcast_dynamic-update-slice_fusion.2
  75.7 1.7 multiply_convert_fusion.2
  77.4 1.1 constant_dynamic-slice_fusion.2
  78.7 0.5 fusion.60
  79.4 0.5 fusion.61
  80.3 1.5 fusion.63
  81.7 3.0 bitcast_dynamic-update-slice_fusion.2
  84.9 13.5 %scatter_custom_fusion = f32[512,512]{1,0:T(8,128)S(1)} fusion(s32[2048]{0:T(1024)} %bitcast.107, f32[2048,512]{1,0:T(8,128)} %bitcast.108, f32[]{:T(128)} %constant.75.clone.1), kind=kCustom, calls=%fused_computation.35 | custom fusion | flops 1048576 | bytes 1049088 | tf_op jit(solution)/shard_map/scatter-add | solution.py:131
  98.4 0.9 convert_element_type.46
  99.4 13.2 %scatter_custom_fusion.1 = f32[24,512]{1,0:T(8,128)S(1)} fusion(s32[2048]{0:T(1024)S(1)} %bitcast.106, f32[2048,512]{1,0:T(8,128)} %bitcast.109, f32[]{:T(128)} %constant.75.clone.1), kind=kCustom, calls=%fused_computation.45 | custom fusion | flops 1048576 | bytes 49664 | tf_op jit(solution)/shard_map/scatter-add | solution.py:125
  112.6 4.8 %collective-permute-start.2 = (f32[8,512]{1,0:T(8,128)S(1)}, f32[8,512]{1,0:T(8,128)S(1)}, u32[]{:S(2)}, u32[]{:S(2)}) collective-permute-start(f32[8,512]{1,0:T(8,128)S(1)} %get-tuple-element.159), channel_id=1, source_target_pairs={{0,4},{4,8},{8,12},{12,16},{16,20},{20,24},{24,28},{1,5},{5,9},{9,... | collective-permute-start | bytes 49160 | tf_op jit(solution)/shard_map/ppermute | solution.py:27
  117.4 1.5 collective-permute-start.3
  118.9 3.8 %reduce_sum.81 = f32[512,512]{1,0:T(8,128)} reduce(f32[4,512,512]{2,1,0:T(8,128)} %get-tuple-element.73, f32[]{:T(128)} %constant.75.clone.1), dimensions={0}, to_apply=%region_15.16 | reduce | flops 786432 | bytes 5242884 | tf_op jit(solution)/shard_map/reduce_sum | solution.py:122
  123.1 1.3 convolution_bitcast_fusion.1
  124.4 2.3 fusion.14
  126.8 20.9 %all-reduce = (f32[512]{0:T(512)S(1)}, f32[512]{0:T(512)S(1)}) all-reduce(f32[512]{0:T(512)S(1)} %reduce_sum.82, f32[512]{0:T(512)S(1)} %reduce_sum.83), channel_id=1, replica_groups=mesh['space'=8,'level'=4] {'space'}, use_global_device_ids=true, to_apply=%region_19.20 | all-reduce | flops 1024 | bytes 8192 | tf_op jit(solution)/shard_map/psum | solution.py:143
  147.7 0.9 convolution_bitcast_fusion.2
  148.6 1.0 fusion.28
  149.6 107.6 %all-reduce.6.cloned.1.call-done = (f32[512,512]{0,1:T(8,128)}, f32[512,512]{1,0:T(8,128)}, f32[512,512]{1,0:T(8,128)}) async-done(((f32[512,512]{0,1:T(8,128)}, f32[512,512]{1,0:T(8,128)}, f32[512,512]{1,0:T(8,128)}), (f32[512,512]{0,1:T(8,128)}, f32[512,512]{1,0:T(8,128)}, f32[512,512]{1,0:T(8,128)})) %all-reduce.6.cloned.1.call-update) | async-done | bytes 3145744 | tf_op jit(solution)/shard_map/psum | solution.py:143
  257.2 59.8 %all-reduce.7 = (bf16[512,512]{0,1:T(8,128)(2,1)S(1)}, bf16[512,512]{1,0:T(8,128)(2,1)}, bf16[512,512]{1,0:T(8,128)(2,1)}, f32[512]{0:T(512)}, f32[512]{0:T(512)}) all-reduce(f32[512,512]{0,1:T(8,128)} %get-tuple-element.143, f32[512,512]{1,0:T(8,128)} %get-tuple-element.144, ...), channel_id=1, replica_groups=mesh['space'=8,'level'=4] {'level'}, use_global_device_ids=true, to_apply=%region_12.13 | all-reduce | flops 787456 | bytes 4726784 | tf_op jit(solution)/shard_map/psum | solution.py:143
  317.0 1.0 copy.21
  (79 shorter events, 5.4 us)
Async XLA Ops:
  7.2 13.3 %copy-start = (bf16[512,512]{1,0:T(8,128)(2,1)S(1)}, bf16[512,512]{1,0:T(8,128)(2,1)}, u32[]{:S(2)}) copy-start(bf16[512,512]{1,0:T(8,128)(2,1)} %param.15) | copy-start | bytes 1572868
  7.2 117.2 %reduce-scatter.2.cloned.1.call-start = ((), (), s32[]{:S(2)}) async-start(), calls=%async_computation.1 | async-start | bytes 655360 | tf_op jit(solution)/shard_map/reduce_scatter | solution.py:134
  8.5 30.0 %collective-permute-start.1 = (bf16[8,512]{1,0:T(8,128)(2,1)S(1)}, bf16[8,512]{1,0:T(8,128)(2,1)S(1)}, u32[]{:S(2)}, u32[]{:S(2)}) collective-permute-start(bf16[8,512]{1,0:T(8,128)(2,1)S(1)} %convolution_convert_fusion), channel_id=1, source_target_pairs={{4,0},{8,4},{12,8},{16,12},{20,16},{24,20},{28,24},{5,1},{9,5},{13... | collective-permute-start | bytes 24584 | tf_op jit(solution)/shard_map/ppermute | solution.py:17
  9.8 28.7 %collective-permute-start = (bf16[8,512]{1,0:T(8,128)(2,1)S(1)}, bf16[8,512]{1,0:T(8,128)(2,1)S(1)}, u32[]{:S(2)}, u32[]{:S(2)}) collective-permute-start(bf16[8,512]{1,0:T(8,128)(2,1)S(1)} %convolution_convert_fusion), channel_id=1, source_target_pairs={{0,4},{4,8},{8,12},{12,16},{16,20},{20,24},{24,28},{1,5},{5,9},{9,... | collective-permute-start | bytes 24584 | tf_op jit(solution)/shard_map/ppermute | solution.py:15
  38.5 9.2 %copy-start.1 = (bf16[512,512]{1,0:T(8,128)(2,1)S(1)}, bf16[512,512]{1,0:T(8,128)(2,1)}, u32[]{:S(2)}) copy-start(bf16[512,512]{1,0:T(8,128)(2,1)} %param.18) | copy-start | bytes 1572868
  38.5 9.2 %copy-start.5 = (f32[512]{0:T(512)S(1)}, f32[512]{0:T(512)}, u32[]{:S(2)}) copy-start(f32[512]{0:T(512)} %param.20) | copy-start | bytes 6148
  38.5 9.2 %copy-start.6 = (f32[512]{0:T(512)S(1)}, f32[512]{0:T(512)}, u32[]{:S(2)}) copy-start(f32[512]{0:T(512)} %param.19) | copy-start | bytes 6148
  84.9 38.2 %copy-start.7 = (bf16[1,8,512]{2,1,0:T(8,128)(2,1)S(1)}, bf16[1,8,512]{2,1,0:T(8,128)(2,1)}, u32[]{:S(2)}) copy-start(bf16[1,8,512]{2,1,0:T(8,128)(2,1)} %param.14) | copy-start | bytes 24580
  99.3 157.9 %all-reduce.6.cloned.1.call-start = ((), (), s32[]{:S(2)}) async-start(), calls=%async_computation.2 | async-start | bytes 6291456 | tf_op jit(solution)/shard_map/psum | solution.py:143
  112.6 10.1 %collective-permute-start.2 = (f32[8,512]{1,0:T(8,128)S(1)}, f32[8,512]{1,0:T(8,128)S(1)}, u32[]{:S(2)}, u32[]{:S(2)}) collective-permute-start(f32[8,512]{1,0:T(8,128)S(1)} %get-tuple-element.159), channel_id=1, source_target_pairs={{0,4},{4,8},{8,12},{12,16},{16,20},{20,24},{24,28},{1,5},{5,9},{9,... | collective-permute-start | bytes 49160 | tf_op jit(solution)/shard_map/ppermute | solution.py:27
  117.4 5.6 %collective-permute-start.3 = (f32[8,512]{1,0:T(8,128)S(1)}, f32[8,512]{1,0:T(8,128)S(1)}, u32[]{:S(2)}, u32[]{:S(2)}) collective-permute-start(f32[8,512]{1,0:T(8,128)S(1)} %get-tuple-element.160), channel_id=1, source_target_pairs={{4,0},{8,4},{12,8},{16,12},{20,16},{24,20},{28,24},{5,1},{9,5},{13... | collective-permute-start | bytes 49160 | tf_op jit(solution)/shard_map/ppermute | solution.py:27
  118.9 28.8 %copy-start.2 = (bf16[512,512]{1,0:T(8,128)(2,1)S(1)}, bf16[512,512]{1,0:T(8,128)(2,1)}, u32[]{:S(2)}) copy-start(bf16[512,512]{1,0:T(8,128)(2,1)} %param.16) | copy-start | bytes 1572868
  122.8 25.8 %copy-start.3 = (bf16[512,512]{1,0:T(8,128)(2,1)S(1)}, bf16[512,512]{1,0:T(8,128)(2,1)}, u32[]{:S(2)}) copy-start(bf16[512,512]{1,0:T(8,128)(2,1)} %param.17) | copy-start | bytes 1572868
  124.4 24.1 %copy-start.4 = (bf16[128,512]{1,0:T(8,128)(2,1)S(1)}, bf16[128,512]{1,0:T(8,128)(2,1)}, u32[]{:S(2)}) copy-start(bf16[128,512]{1,0:T(8,128)(2,1)} %reduce-scatter.2.cloned.1.call-done) | copy-start | bytes 393220
Sparse Core Ops, SparseCore 0:
  99.4 23.2 reduce-scatter.1
  126.9 130.2 all-reduce.5
